TPU v7x, 128 devices: a whole 4x4x4 slice. The times are simulated.
128 devices in a mesh: gx: 4 (over z_lo, core), gy: 8 (over z_hi, y), gz: 4 (over x).
Axes of the slice: x: 4, y: 4, z: 4 (z_hi: 2, z_lo: 2; z = z_hi * 2 + z_lo), core: 2. Of those that a mesh axis runs over, the one named last changes fastest.
Arguments:
- cell_volume: float32 [64, 128, 512], P('gx', 'gy', 'gz'), may hold values from 0.5 to 2
- exponent: int32 [64, 128, 512], P('gx', 'gy', 'gz'), may hold values from 0 to 7
- owner_row: int32 [32768], P(('gx', 'gy', 'gz')), may hold values from 0 to 32767, as said below
Outputs:
- stencil_out: float32 [27, 32768, 128], P(None, ('gx', 'gy', 'gz'))
- lumped_out: float32 [32768, 128], P(('gx', 'gy', 'gz'))
Inputs may be any that keep to these rules, and one draw needn't show every extreme that they name: owner_row is a permutation of the row blocks; the row blocks of each device's share of owner_row go to each owner (owner_row // 256) exactly 2 times.
All inputs are finite; a program needn't handle non-finite values.
Results may differ from a plain program's by a relative error of at most 0.00007.
Values sent between devices are 32-bit elements; how exact they have to be, the bound alone decides.
A program may use at most 64 MiB of HBM per device.

v0:
```python
import jax
import jax.numpy as jnp
import numpy as np
from jax import lax
from jax.sharding import PartitionSpec as P

log_step = 0.3


def from_behind(block, axis, distance):
    devices = range(lax.axis_size(axis))
    route = [((i - distance) % len(devices), i) for i in devices]
    return lax.ppermute(block, axis, route)


def weight_table():
    table = np.zeros((27, 8), np.float32)
    for index_o in range(27):
        offsets = (index_o // 9 - 1, index_o // 3 % 3 - 1, index_o % 3 - 1)
        for index_a in range(8):
            corner = (index_a // 4, index_a // 2 % 2, index_a % 2)
            inside = all((0 <= corner[slot_d] + offsets[slot_d] <= 1 for slot_d in range(3)))
            factor = 1.0
            for slot_d in range(3):
                factor = factor * (2.0 if offsets[slot_d] == 0 else 1.0)
            table[index_o, index_a] = factor / 64.0 if inside else 0.0
    return table


def rim_section(current, along, stack_at, sender):
    length = current.shape[along]
    interior = lax.slice_in_dim(current, 0, length - 1, axis=along)
    top_layer = lax.slice_in_dim(current, length - 1, length, axis=along)
    received = sender(top_layer)
    behind = jnp.concatenate([received, interior], axis=along)
    return jnp.stack([current, behind], axis=stack_at)


def shards(cell_volume, exponent, owner_row):
    weight = cell_volume * jnp.exp(-log_step * exponent.astype(jnp.float32))
    span_x, span_y, span_z = weight.shape
    line_count = span_x * span_y
    devices_all = lax.axis_size(("gx", "gy", "gz"))

    def send_z(rim_layer):
        return from_behind(rim_layer, "gz", 1)

    def send_x(rim_layer):
        return from_behind(rim_layer, "gx", 1)

    def send_y(rim_layer):
        return from_behind(rim_layer, "gy", 1)

    owner_dev = owner_row // line_count
    by_owner = jnp.argsort(owner_dev, stable=True)
    slot_ids = (owner_row % line_count)[by_owner].reshape(1, devices_all, -1)
    table = jnp.asarray(weight_table())
    sectioned_z = rim_section(weight, 2, 0, send_z)
    sectioned_x = rim_section(sectioned_z, 1, 0, send_x)
    sectioned_all = rim_section(sectioned_x, 3, 1, send_y)
    corners = sectioned_all.reshape(8, line_count, span_z)
    packed = corners[:, by_owner].reshape(8, devices_all, -1, span_z)
    got_rows, got_slots = (
        lax.all_to_all(packed, ("gx", "gy", "gz"), split_axis=1, concat_axis=1, tiled=True),
        lax.all_to_all(slot_ids, ("gx", "gy", "gz"), split_axis=1, concat_axis=1, tiled=True),
    )
    placing = jnp.argsort(got_slots.reshape(-1))
    placed = got_rows.reshape(8, line_count, span_z)[:, placing]
    stencil_rows = jnp.einsum("oa,alz->olz", table, placed, precision=lax.Precision.HIGHEST)
    lumped_rows = 1.0 / jnp.sum(stencil_rows, axis=0)
    return (stencil_rows, lumped_rows)


def solution(mesh):
    return jax.shard_map(
        shards,
        mesh=mesh,
        in_specs=(P("gx", "gy", "gz"), P("gx", "gy", "gz"), P(("gx", "gy", "gz"))),
        out_specs=(P(None, ("gx", "gy", "gz"), None), P(("gx", "gy", "gz"), None)),
        check_vma=False,
    )
```

profile of v0, /device:TPU:1, one launch (start us, length us, event | category | flops | bytes accessed | tf_op | source)
XLA Modules:
  0.0 70.4 jit_solution(13474387986052149990)
XLA Ops:
  0.6 1.0 %exponential_multiply_fusion = f32[16,16,128]{2,1,0:T(8,128)S(1)} fusion(f32[16,16,128]{2,1,0:T(8,128)} %param.4, s32[16,16,128]{2,1,0:T(8,128)} %param.5), kind=kLoop, calls=%fused_computation.23 | loop fusion | flops 98304 | bytes 393216 | tf_op jit(solution)/shard_map/mul | solution.py:40
  1.6 0.1 slice.30
  1.7 2.1 %collective-permute-start = (f32[16,16,1]{2,1,0:T(8,128)S(1)}, f32[16,16,1]{2,1,0:T(8,128)S(1)}, u32[]{:S(2)}, u32[]{:S(2)}) collective-permute-start(f32[16,16,1]{2,1,0:T(8,128)S(1)} %slice.30), channel_id=1, source_target_pairs={{3,0},{0,1},{1,2},{2,3},{7,4},{4,5},{5,6},{6,7},{11,8},{8,9},{9,10... | collective-permute-start | bytes 3080 | tf_op jit(solution)/shard_map/ppermute | solution.py:13
  3.8 0.7 and_select_fusion
  4.5 3.2 %sort.34 = (s32[256]{0:T(256)}, s32[256]{0:T(256)S(1)}) sort(s32[256]{0:T(256)S(1)} %get-tuple-element.13, s32[256]{0:T(256)S(1)} %iota.8), dimensions={0}, to_apply=%region_0.1 | sort | flops 2048 | bytes 4096 | tf_op jit(solution)/shard_map/jit(argsort)/sort | solution.py:55
  7.7 1.9 %gather_fusion.1 = s32[256]{0:T(256)S(1)} fusion(s32[256]{0:T(256)S(1)} %get-tuple-element.12, s32[1024]{0:T(1024)S(1)} %pad_clamp_fusion.1), kind=kCustom, calls=%fused_computation.1 | custom fusion | bytes 3072 | tf_op jit(solution)/shard_map/gather | solution.py:56
  9.6 0.8 %reshape.22 = s32[1,128,2]{2,1,0:T(8,128)} reshape(s32[256]{0:T(256)S(1)} %gather_fusion.1) | data formatting | bytes 2048 | tf_op jit(solution)/shard_map/reshape | solution.py:56
  10.4 10.7 %all-to-all-start.1 = ((s32[1,128,2]{2,0,1:T(1,128)}), s32[1,128,2]{2,0,1:T(1,128)S(1)}, u32[]{:S(2)}, u32[]{:S(2)}) async-start(s32[1,128,2]{2,0,1:T(1,128)} %bitcast.12), calls=%async_computation.1 | async-start | bytes 131072 | tf_op jit(solution)/shard_map/all_to_all | solution.py:65
  21.1 0.0 collective-permute-done
  21.1 0.1 maximum_bitcast_fusion.2
  21.2 1.8 %collective-permute-start.1 = (f32[2,1,16,128]{3,2,1,0:T(8,128)S(1)}, f32[2,1,16,128]{3,2,1,0:T(8,128)S(1)}, u32[]{:S(2)}, u32[]{:S(2)}) collective-permute-start(f32[2,1,16,128]{3,2,1,0:T(8,128)S(1)} %fusion.7), channel_id=1, source_target_pairs={{96,0},{0,32},{32,64},{64,96},{97,1},{1,33},{33,65},{65,97},{98,2}... | collective-permute-start | bytes 49160 | tf_op jit(solution)/shard_map/ppermute | solution.py:13
  23.1 0.8 %collective-permute-done.1 = f32[2,1,16,128]{3,2,1,0:T(8,128)S(1)} collective-permute-done((f32[2,1,16,128]{3,2,1,0:T(8,128)S(1)}, f32[2,1,16,128]{3,2,1,0:T(8,128)S(1)}, u32[]{:S(2)}, u32[]{:S(2)}) %collective-permute-start.1) | collective-permute-done | bytes 16416 | tf_op jit(solution)/shard_map/ppermute | solution.py:13
  24.0 1.3 %collective-permute-start.2 = (f32[2,2,16,1,128]{4,3,2,1,0:T(1,128)S(1)}, f32[2,2,16,1,128]{4,3,2,1,0:T(1,128)S(1)}, u32[]{:S(2)}, u32[]{:S(2)}) collective-permute-start(f32[2,2,16,1,128]{4,3,2,1,0:T(1,128)S(1)} %fusion.6), channel_id=1, source_target_pairs={{28,0},{0,4},{4,8},{8,12},{12,16},{16,20},{20,24},{24,28},{29,1},{... | collective-permute-start | bytes 98312 | tf_op jit(solution)/shard_map/ppermute | solution.py:13
  25.4 5.6 %collective-permute-done.2 = f32[2,2,16,1,128]{4,3,2,1,0:T(1,128)S(1)} collective-permute-done((f32[2,2,16,1,128]{4,3,2,1,0:T(1,128)S(1)}, f32[2,2,16,1,128]{4,3,2,1,0:T(1,128)S(1)}, u32[]{:S(2)}, u32[]{:S(2)}) %collective-permute-start.2) | collective-permute-done | bytes 32800 | tf_op jit(solution)/shard_map/ppermute | solution.py:13
  31.0 0.1 maximum_bitcast_fusion
  31.0 0.1 pad_maximum_fusion
  31.1 0.0 copy-start
  31.1 0.6 copy.11
  31.7 2.0 %gather_fusion = f32[256,8,128]{2,1,0:T(8,128)} fusion(f32[8,256,128]{2,0,1:T(8,128)S(1)} %copy.11, s32[1024]{0:T(1024)S(1)} %pad_clamp_fusion.1), kind=kCustom, calls=%fused_computation | custom fusion | bytes 2098176 | tf_op jit(solution)/shard_map/gather | solution.py:62
  33.7 0.0 all-to-all-done.1
  33.7 8.5 %all-to-all-start = ((f32[8,128,2,128]{3,0,2,1:T(8,128)}), f32[8,128,2,128]{3,0,2,1:T(8,128)S(1)}, u32[]{:S(2)}, u32[]{:S(2)}) async-start(f32[8,128,2,128]{3,0,2,1:T(8,128)} %bitcast.10), calls=%async_computation | async-start | bytes 2097152 | tf_op jit(solution)/shard_map/all_to_all | solution.py:64
  42.2 0.5 broadcast.50
  42.7 0.8 %reduce.3 = s32[128,2]{1,0:T(8,128)S(1)} reduce(s32[1,128,2]{2,0,1:T(1,128)S(1)} %all-to-all-done.1, s32[]{:T(128)} %broadcast.50), dimensions={0}, to_apply=%all_to_all.7.reduce_sub_computation.3 | reduce | bytes 2052 | tf_op jit(solution)/shard_map/all_to_all | solution.py:65
  43.6 0.1 reshape.23
  43.7 3.2 %sort.35 = (s32[256]{0:T(256)}, s32[256]{0:T(256)S(1)}) sort(s32[256]{0:T(256)S(1)} %reshape.23, s32[256]{0:T(256)S(1)} %iota.9), dimensions={0}, to_apply=%region_1.2 | sort | flops 2048 | bytes 4096 | tf_op jit(solution)/shard_map/jit(argsort)/sort | solution.py:67
  46.9 14.2 %all-to-all-done = f32[8,128,2,128]{3,0,2,1:T(8,128)S(1)} async-done(((f32[8,128,2,128]{3,0,2,1:T(8,128)}), f32[8,128,2,128]{3,0,2,1:T(8,128)S(1)}, u32[]{:S(2)}, u32[]{:S(2)}) %all-to-all-start) | async-done | bytes 1048608 | tf_op jit(solution)/shard_map/all_to_all | solution.py:64
  61.1 1.0 %gather_fusion.2 = f32[256,8,128]{2,1,0:T(8,128)S(1)} fusion(f32[8,256,128]{2,0,1:T(8,128)S(1)} %bitcast.33, s32[1024]{0:T(1024)S(1)} %pad_clamp_fusion), kind=kCustom, calls=%fused_computation.2 | custom fusion | bytes 2098176 | tf_op jit(solution)/shard_map/gather | solution.py:68
  62.1 0.0 copy-done
  62.1 3.7 %fusion.8 = (f32[256,128]{1,0:T(8,128)S(1)}, f32[27,256,128]{2,0,1:T(8,128)S(1)}) fusion(f32[27,8,1]{0,1,2:T(8,128)S(1)} %copy-done, f32[256,8,128]{2,1,0:T(8,128)S(1)} %gather_fusion.2), kind=kOutput, calls=%fused_computation.38 | convolution fusion | flops 85786624 | bytes 4719456 | tf_op jit(solution)/shard_map/oa,alz->olz/dot_general | solution.py:69
  65.9 0.7 broadcast_divide_fusion
  66.5 3.8 %copy.13 = f32[27,256,128]{2,1,0:T(8,128)} copy(f32[27,256,128]{2,0,1:T(8,128)S(1)} %get-tuple-element.15) | data formatting | bytes 7077888
  (13 shorter events, 0.2 us)
Async XLA Ops:
  1.7 19.4 %collective-permute-start = (f32[16,16,1]{2,1,0:T(8,128)S(1)}, f32[16,16,1]{2,1,0:T(8,128)S(1)}, u32[]{:S(2)}, u32[]{:S(2)}) collective-permute-start(f32[16,16,1]{2,1,0:T(8,128)S(1)} %slice.30), channel_id=1, source_target_pairs={{3,0},{0,1},{1,2},{2,3},{7,4},{4,5},{5,6},{6,7},{11,8},{8,9},{9,10... | collective-permute-start | bytes 3080 | tf_op jit(solution)/shard_map/ppermute | solution.py:13
  10.4 23.3 %all-to-all-start.1 = ((s32[1,128,2]{2,0,1:T(1,128)}), s32[1,128,2]{2,0,1:T(1,128)S(1)}, u32[]{:S(2)}, u32[]{:S(2)}) async-start(s32[1,128,2]{2,0,1:T(1,128)} %bitcast.12), calls=%async_computation.1 | async-start | bytes 131072 | tf_op jit(solution)/shard_map/all_to_all | solution.py:65
  21.2 2.7 %collective-permute-start.1 = (f32[2,1,16,128]{3,2,1,0:T(8,128)S(1)}, f32[2,1,16,128]{3,2,1,0:T(8,128)S(1)}, u32[]{:S(2)}, u32[]{:S(2)}) collective-permute-start(f32[2,1,16,128]{3,2,1,0:T(8,128)S(1)} %fusion.7), channel_id=1, source_target_pairs={{96,0},{0,32},{32,64},{64,96},{97,1},{1,33},{33,65},{65,97},{98,2}... | collective-permute-start | bytes 49160 | tf_op jit(solution)/shard_map/ppermute | solution.py:13
  24.0 6.9 %collective-permute-start.2 = (f32[2,2,16,1,128]{4,3,2,1,0:T(1,128)S(1)}, f32[2,2,16,1,128]{4,3,2,1,0:T(1,128)S(1)}, u32[]{:S(2)}, u32[]{:S(2)}) collective-permute-start(f32[2,2,16,1,128]{4,3,2,1,0:T(1,128)S(1)} %fusion.6), channel_id=1, source_target_pairs={{28,0},{0,4},{4,8},{8,12},{12,16},{16,20},{20,24},{24,28},{29,1},{... | collective-permute-start | bytes 98312 | tf_op jit(solution)/shard_map/ppermute | solution.py:13
  31.1 31.0 %copy-start = (f32[27,8,1]{0,1,2:T(8,128)S(1)}, f32[27,8,1]{0,1,2:T(8,128)}, u32[]{:S(2)}) copy-start(f32[27,8,1]{0,1,2:T(8,128)} %constant.39) | copy-start | bytes 2596
  33.7 27.3 %all-to-all-start = ((f32[8,128,2,128]{3,0,2,1:T(8,128)}), f32[8,128,2,128]{3,0,2,1:T(8,128)S(1)}, u32[]{:S(2)}, u32[]{:S(2)}) async-start(f32[8,128,2,128]{3,0,2,1:T(8,128)} %bitcast.10), calls=%async_computation | async-start | bytes 2097152 | tf_op jit(solution)/shard_map/all_to_all | solution.py:64
where the time goes:
time: 70.6 us; the launch traced here: 70.4 us
  starting transfers between devices  24.4 us (35%)
  waiting for transfers between devices  20.6 us (29%)
  local copies, waits for them, and re-layouts  10.9 us (15%)
  other arithmetic  9.93 us (14%)
  matrix products  3.73 us (5%)
  between operations  0.8 us (1%)
    all_to_all x1, waiting for transfers between devices, shards(): lax.all_to_all(packed, ('gx', 'gy', 'gz'), split_axis=1, concat_axis=1, t...  14.2 us
    all_to_all x1, starting transfers between devices, shards(): lax.all_to_all(slot_ids, ('gx', 'gy', 'gz'), split_axis=1, concat_axis=1,...  10.7 us
    all_to_all x1, starting transfers between devices, shards(): lax.all_to_all(packed, ('gx', 'gy', 'gz'), split_axis=1, concat_axis=1, t...  8.48 us
    ppermute x3, waiting for transfers between devices, from_behind(): return lax.ppermute(block, axis, route)  6.43 us
    ppermute x3, starting transfers between devices, from_behind(): return lax.ppermute(block, axis, route)  5.24 us
    unnamed x3, local copies, waits for them, and re-layouts  3.85 us
    dot_general x1, matrix products, shards(): jnp.einsum('oa,alz->olz', table, placed, precision=lax.Precision.HIGHEST)  3.73 us
    sort x1, other arithmetic, shards(): by_owner = jnp.argsort(owner_dev, stable=True)  3.17 us
  transfers between devices with their start and end apart: 5, of which 3 were waited for; matrix products, arithmetic and copies ran while one was open for 20% of the time, Pallas kernels for 0%

commit v1 on v0

--- a/solution.py
+++ b/solution.py
@@ -61,7 +61,15 @@
     corners = sectioned_all.reshape(8, line_count, span_z)
     packed = corners[:, by_owner].reshape(8, devices_all, -1, span_z)
     got_rows, got_slots = (
-        lax.all_to_all(packed, ("gx", "gy", "gz"), split_axis=1, concat_axis=1, tiled=True),
+        jnp.concatenate(
+            lax.all_to_all(
+                jnp.stack(jnp.split(packed, lax.axis_size(("gx", "gy", "gz")), axis=1)),
+                ("gx", "gy", "gz"),
+                0,
+                0,
+            ),
+            axis=1,
+        ),
         lax.all_to_all(slot_ids, ("gx", "gy", "gz"), split_axis=1, concat_axis=1, tiled=True),
     )
     placing = jnp.argsort(got_slots.reshape(-1))

time: 70.6 us -> 146 us (2.07)
  local copies, waits for them, and re-layouts: 10.9 us -> 86.6 us
    unnamed x3 -> x130, local copies, waits for them, and re-layouts: 3.85 us -> 79.9 us
  transfers between devices with their start and end apart: 5 -> 5, of which waited for: 3 -> 3; matrix products, arithmetic and copies ran while one was open for 20% -> 62% of each run, Pallas kernels for 0% -> 0%
where the time goes in v1:
time: 146 us
  local copies, waits for them, and re-layouts  86.6 us (59%)
  starting transfers between devices  24.4 us (17%)
  waiting for transfers between devices  20.6 us (14%)
  other arithmetic  9.93 us (7%)
  matrix products  3.72 us (3%)
    unnamed x130, local copies, waits for them, and re-layouts  79.9 us
    all_to_all x1, waiting for transfers between devices, shards(): lax.all_to_all(jnp.stack(jnp.split(packed, lax.axis_size(('gx', 'gy', 'gz...  14.2 us
    all_to_all x1, starting transfers between devices, shards(): lax.all_to_all(slot_ids, ('gx', 'gy', 'gz'), split_axis=1, concat_axis=1,...  10.7 us
    all_to_all x1, starting transfers between devices, shards(): lax.all_to_all(jnp.stack(jnp.split(packed, lax.axis_size(('gx', 'gy', 'gz...  8.49 us
    ppermute x3, waiting for transfers between devices, from_behind(): return lax.ppermute(block, axis, route)  6.43 us
    ppermute x3, starting transfers between devices, from_behind(): return lax.ppermute(block, axis, route)  5.24 us
    dot_general x1, matrix products, shards(): jnp.einsum('oa,alz->olz', table, placed, precision=lax.Precision.HIGHEST)  3.72 us
    sort x1, other arithmetic, shards(): by_owner = jnp.argsort(owner_dev, stable=True)  3.17 us
  transfers between devices with their start and end apart: 5, of which 3 were waited for; matrix products, arithmetic and copies ran while one was open for 62% of the time, Pallas kernels for 0%

profile of v1, /device:TPU:1, one launch (start us, length us, event | category | flops | bytes accessed | tf_op | source)
XLA Modules:
  0.0 146.1 jit_solution(7556392448466282280)
XLA Ops:
  0.6 1.0 exponential_multiply_fusion
  1.7 2.1 %collective-permute-start = (f32[16,16,1]{2,1,0:T(8,128)S(1)}, f32[16,16,1]{2,1,0:T(8,128)S(1)}, u32[]{:S(2)}, u32[]{:S(2)}) collective-permute-start(f32[16,16,1]{2,1,0:T(8,128)S(1)} %slice.30), channel_id=1, source_target_pairs={{3,0},{0,1},{1,2},{2,3},{7,4},{4,5},{5,6},{6,7},{11,8},{8,9},{9,10... | collective-permute-start | bytes 3080 | tf_op jit(solution)/shard_map/ppermute | solution.py:13
  3.8 0.7 and_select_fusion
  4.5 3.2 %sort.34 = (s32[256]{0:T(256)}, s32[256]{0:T(256)S(1)}) sort(s32[256]{0:T(256)S(1)} %get-tuple-element.13, s32[256]{0:T(256)S(1)} %iota.8), dimensions={0}, to_apply=%region_0.1 | sort | flops 2048 | bytes 4096 | tf_op jit(solution)/shard_map/jit(argsort)/sort | solution.py:55
  7.7 1.9 %gather_fusion.1 = s32[256]{0:T(256)S(1)} fusion(s32[256]{0:T(256)S(1)} %get-tuple-element.12, s32[1024]{0:T(1024)S(1)} %pad_clamp_fusion.1), kind=kCustom, calls=%fused_computation.1 | custom fusion | bytes 3072 | tf_op jit(solution)/shard_map/gather | solution.py:56
  9.6 0.8 reshape.22
  10.4 10.7 %all-to-all-start.1 = ((s32[1,128,2]{2,0,1:T(1,128)}), s32[1,128,2]{2,0,1:T(1,128)S(1)}, u32[]{:S(2)}, u32[]{:S(2)}) async-start(s32[1,128,2]{2,0,1:T(1,128)} %bitcast.143), calls=%async_computation.1 | async-start | bytes 131072 | tf_op jit(solution)/shard_map/all_to_all | solution.py:73
  21.2 1.8 %collective-permute-start.1 = (f32[2,1,16,128]{3,2,1,0:T(8,128)S(1)}, f32[2,1,16,128]{3,2,1,0:T(8,128)S(1)}, u32[]{:S(2)}, u32[]{:S(2)}) collective-permute-start(f32[2,1,16,128]{3,2,1,0:T(8,128)S(1)} %fusion.7), channel_id=1, source_target_pairs={{96,0},{0,32},{32,64},{64,96},{97,1},{1,33},{33,65},{65,97},{98,2}... | collective-permute-start | bytes 49160 | tf_op jit(solution)/shard_map/ppermute | solution.py:13
  23.1 0.8 collective-permute-done.1
  24.0 1.3 collective-permute-start.2
  25.4 5.6 %collective-permute-done.2 = f32[2,2,16,1,128]{4,3,2,1,0:T(1,128)S(1)} collective-permute-done((f32[2,2,16,1,128]{4,3,2,1,0:T(1,128)S(1)}, f32[2,2,16,1,128]{4,3,2,1,0:T(1,128)S(1)}, u32[]{:S(2)}, u32[]{:S(2)}) %collective-permute-start.2) | collective-permute-done | bytes 32800 | tf_op jit(solution)/shard_map/ppermute | solution.py:13
  31.1 0.6 copy.265
  31.7 1.0 gather_fusion
  32.8 0.6 constant_dynamic-update-slice_fusion.127
  33.4 0.6 constant_dynamic-update-slice_fusion.126
  34.0 0.6 constant_dynamic-update-slice_fusion.125
  35.8 0.6 constant_dynamic-update-slice_fusion.122
  37.6 0.6 constant_dynamic-update-slice_fusion.119
  39.4 0.6 constant_dynamic-update-slice_fusion.116
  41.2 0.6 constant_dynamic-update-slice_fusion.113
  43.0 0.6 constant_dynamic-update-slice_fusion.110
  44.8 0.6 constant_dynamic-update-slice_fusion.107
  45.4 0.6 constant_dynamic-update-slice_fusion.106
  47.2 0.6 constant_dynamic-update-slice_fusion.103
  49.0 0.6 constant_dynamic-update-slice_fusion.100
  50.8 0.6 constant_dynamic-update-slice_fusion.97
  52.6 0.6 constant_dynamic-update-slice_fusion.94
  54.4 0.6 constant_dynamic-update-slice_fusion.91
  56.2 0.6 constant_dynamic-update-slice_fusion.88
  56.8 0.6 constant_dynamic-update-slice_fusion.87
  58.6 0.6 constant_dynamic-update-slice_fusion.84
  60.4 0.6 constant_dynamic-update-slice_fusion.81
  62.2 0.6 constant_dynamic-update-slice_fusion.78
  64.0 0.6 constant_dynamic-update-slice_fusion.75
  65.8 0.6 constant_dynamic-update-slice_fusion.72
  67.6 0.6 constant_dynamic-update-slice_fusion.69
  68.2 0.6 constant_dynamic-update-slice_fusion.68
  70.0 0.6 constant_dynamic-update-slice_fusion.65
  71.8 0.6 constant_dynamic-update-slice_fusion.62
  73.5 0.6 constant_dynamic-update-slice_fusion.59
  75.3 0.6 constant_dynamic-update-slice_fusion.56
  77.1 0.6 constant_dynamic-update-slice_fusion.53
  78.9 0.6 constant_dynamic-update-slice_fusion.50
  79.5 0.6 constant_dynamic-update-slice_fusion.49
  81.3 0.6 constant_dynamic-update-slice_fusion.46
  83.1 0.6 constant_dynamic-update-slice_fusion.43
  84.9 0.6 constant_dynamic-update-slice_fusion.40
  86.7 0.6 constant_dynamic-update-slice_fusion.37
  88.5 0.6 constant_dynamic-update-slice_fusion.34
  90.3 0.6 constant_dynamic-update-slice_fusion.31
  90.9 0.6 constant_dynamic-update-slice_fusion.30
  92.7 0.6 constant_dynamic-update-slice_fusion.27
  94.5 0.6 constant_dynamic-update-slice_fusion.24
  96.3 0.6 constant_dynamic-update-slice_fusion.21
  98.1 0.6 constant_dynamic-update-slice_fusion.18
  99.9 0.6 constant_dynamic-update-slice_fusion.15
  109.5 8.5 %all-to-all-start = ((f32[128,8,1,2,128]{4,1,3,2,0:T(8,128)}), f32[128,8,1,2,128]{4,1,3,2,0:T(8,128)S(1)}, u32[]{:S(2)}, u32[]{:S(2)}) async-start(f32[128,8,1,2,128]{4,1,3,2,0:T(8,128)} %constant_dynamic-update-slice_fusion), calls=%async_computation | async-start | bytes 2097152 | tf_op jit(solution)/shard_map/all_to_all | solution.py:65
  118.5 0.8 reduce.3
  119.5 3.2 %sort.35 = (s32[256]{0:T(256)}, s32[256]{0:T(256)S(1)}) sort(s32[256]{0:T(256)S(1)} %reshape.23, s32[256]{0:T(256)S(1)} %iota.9), dimensions={0}, to_apply=%region_1.2 | sort | flops 2048 | bytes 4096 | tf_op jit(solution)/shard_map/jit(argsort)/sort | solution.py:75
  122.7 14.2 %all-to-all-done = f32[128,8,1,2,128]{4,1,3,2,0:T(8,128)S(1)} async-done(((f32[128,8,1,2,128]{4,1,3,2,0:T(8,128)}), f32[128,8,1,2,128]{4,1,3,2,0:T(8,128)S(1)}, u32[]{:S(2)}, u32[]{:S(2)}) %all-to-all-start) | async-done | bytes 1048608 | tf_op jit(solution)/shard_map/all_to_all | solution.py:65
  136.8 1.0 gather_fusion.2
  137.9 3.7 %fusion.8 = (f32[256,128]{1,0:T(8,128)S(1)}, f32[27,256,128]{2,0,1:T(8,128)S(1)}) fusion(f32[27,8,1]{0,1,2:T(8,128)S(1)} %copy-done, f32[256,8,128]{2,1,0:T(8,128)S(1)} %gather_fusion.2), kind=kOutput, calls=%fused_computation.294 | convolution fusion | flops 85786624 | bytes 4719456 | tf_op jit(solution)/shard_map/oa,alz->olz/dot_general | solution.py:77
  141.6 0.7 broadcast_divide_fusion
  142.3 3.8 %copy.268 = f32[27,256,128]{2,1,0:T(8,128)} copy(f32[27,256,128]{2,0,1:T(8,128)S(1)} %get-tuple-element.15) | data formatting | bytes 7077888
  (108 shorter events, 52.1 us)
Async XLA Ops:
  1.7 19.4 %collective-permute-start = (f32[16,16,1]{2,1,0:T(8,128)S(1)}, f32[16,16,1]{2,1,0:T(8,128)S(1)}, u32[]{:S(2)}, u32[]{:S(2)}) collective-permute-start(f32[16,16,1]{2,1,0:T(8,128)S(1)} %slice.30), channel_id=1, source_target_pairs={{3,0},{0,1},{1,2},{2,3},{7,4},{4,5},{5,6},{6,7},{11,8},{8,9},{9,10... | collective-permute-start | bytes 3080 | tf_op jit(solution)/shard_map/ppermute | solution.py:13
  10.4 99.1 %all-to-all-start.1 = ((s32[1,128,2]{2,0,1:T(1,128)}), s32[1,128,2]{2,0,1:T(1,128)S(1)}, u32[]{:S(2)}, u32[]{:S(2)}) async-start(s32[1,128,2]{2,0,1:T(1,128)} %bitcast.143), calls=%async_computation.1 | async-start | bytes 131072 | tf_op jit(solution)/shard_map/all_to_all | solution.py:73
  21.2 2.7 %collective-permute-start.1 = (f32[2,1,16,128]{3,2,1,0:T(8,128)S(1)}, f32[2,1,16,128]{3,2,1,0:T(8,128)S(1)}, u32[]{:S(2)}, u32[]{:S(2)}) collective-permute-start(f32[2,1,16,128]{3,2,1,0:T(8,128)S(1)} %fusion.7), channel_id=1, source_target_pairs={{96,0},{0,32},{32,64},{64,96},{97,1},{1,33},{33,65},{65,97},{98,2}... | collective-permute-start | bytes 49160 | tf_op jit(solution)/shard_map/ppermute | solution.py:13
  24.0 6.9 %collective-permute-start.2 = (f32[2,2,16,1,128]{4,3,2,1,0:T(1,128)S(1)}, f32[2,2,16,1,128]{4,3,2,1,0:T(1,128)S(1)}, u32[]{:S(2)}, u32[]{:S(2)}) collective-permute-start(f32[2,2,16,1,128]{4,3,2,1,0:T(1,128)S(1)} %fusion.6), channel_id=1, source_target_pairs={{28,0},{0,4},{4,8},{8,12},{12,16},{16,20},{20,24},{24,28},{29,1},{... | collective-permute-start | bytes 98312 | tf_op jit(solution)/shard_map/ppermute | solution.py:13
  31.7 106.1 %copy-start = (f32[27,8,1]{0,1,2:T(8,128)S(1)}, f32[27,8,1]{0,1,2:T(8,128)}, u32[]{:S(2)}) copy-start(f32[27,8,1]{0,1,2:T(8,128)} %constant.39) | copy-start | bytes 2596
  109.5 27.3 %all-to-all-start = ((f32[128,8,1,2,128]{4,1,3,2,0:T(8,128)}), f32[128,8,1,2,128]{4,1,3,2,0:T(8,128)S(1)}, u32[]{:S(2)}, u32[]{:S(2)}) async-start(f32[128,8,1,2,128]{4,1,3,2,0:T(8,128)} %constant_dynamic-update-slice_fusion), calls=%async_computation | async-start | bytes 2097152 | tf_op jit(solution)/shard_map/all_to_all | solution.py:65
